TPU v7x, 128 devices: a whole 4x4x4 slice. The times are simulated.
128 devices in a mesh: grp: 2 (over z_lo), ang: 64 (over z_hi, x, y, core).
Axes of the slice: x: 4, y: 4, z: 4 (z_hi: 2, z_lo: 2; z = z_hi * 2 + z_lo), core: 2. Of those that a mesh axis runs over, the one named last changes fastest.
Arguments:
- children: bfloat16 [2, 128, 8, 2, 1, 8192], P(None, ('grp', 'ang')), may hold values from -6 to 6
- present: int32 [128, 8], P(('grp', 'ang')), may hold values 0 or 1
- interp: float32 [8, 32768], replicated, may hold values from -2 to 2
- phase: float32 [8, 32768], replicated, may hold values from -3.140625 to 3.140625
- trans: float32 [2, 316, 32768], P(None, None, 'ang'), may hold values from -0.6 to 0.6
- sources: int32 [128, 8], P('grp'), may hold values from 0 to 127
- trans_ids: int32 [128, 8], P('grp'), may hold values from 0 to 315
- list_len: int32 [128], P('grp'), may hold values from 1 to 8
Outputs:
- received: float32 [2, 128, 2, 1, 32768], P(None, 'grp', None, None, 'ang')
All inputs are finite; a program needn't handle non-finite values. No bound on the sum of `present` on one device may be relied on, other than what follows from the above.
Results may differ from a plain program's by a relative error of at most 0.0029.
Values may be sent and summed in bfloat16 or wider, within the bound.
No kernel may reach another device: no remote copies, remote signals or barrier semaphores. Data moves between devices by JAX's collectives and lax.ppermute only.
A program may use at most 128 MiB of HBM per device.

v0:
```python
import jax
import jax.numpy as jnp
from jax import lax
from jax.sharding import Mesh
from jax.sharding import PartitionSpec as P

HW = 4
ANG = ("ang_0", "ang_1", "ang_2", "ang_3")
GRP_ANG = ("grp", "ang_0", "ang_1", "ang_2", "ang_3")


def in_blocks(value, dim, length):
    before, after = (value.shape[:dim], value.shape[dim + 1 :])
    return jnp.moveaxis(value.reshape(*before, length, -1, *after), dim, 0)


def in_order(parts, dim):
    lengths = list(parts.shape[1:])
    lengths[dim] *= parts.shape[0]
    return jnp.moveaxis(parts, 0, dim).reshape(lengths)


def exchange_in_order(parts, axes, sequence):
    lengths = [lax.axis_size(a) for a in axes]
    parts = parts.reshape(*lengths, *parts.shape[1:])
    for k in sequence:
        parts = lax.all_to_all(parts, axes[k], split_axis=k, concat_axis=k, tiled=True)
    return parts.reshape(-1, *parts.shape[len(axes) :])


def two_step_exchange(value, groups, sequence, split_dim, concat_dim):
    length = lax.axis_size(groups[0]) * lax.axis_size(groups[1])
    parts = in_blocks(value, split_dim, length)
    return in_order(exchange_in_order(parts, groups, sequence), concat_dim)


def extended_2(block, sides, width):
    for axis, dim in sides:
        count = lax.axis_size(axis)
        forward = [(i, i + 1) for i in range(count - 1)]
        forward.append((count - 1, 0))
        backward = [(target, source) for source, target in forward]
        low = lax.ppermute(
            lax.slice_in_dim(block, block.shape[dim] - width, None, axis=dim), axis, forward
        )
        high = lax.ppermute(lax.slice_in_dim(block, 0, width, axis=dim), axis, backward)
        block = jnp.concatenate([low, block, high], axis=dim)
    return block


def sent_to_all(value, axis):
    length = lax.axis_size(axis)
    return lax.all_to_all(
        jnp.broadcast_to(value[None], (length, *value.shape)), axis, 0, 0, tiled=True
    )


def gathered_copies(value, axis, dim):
    return in_order(sent_to_all(value, axis), dim)


def aggregate(extended, weights, cosine, sine_part, coarse_len):
    taps_count = weights.shape[0]
    octants = extended.shape[2]
    fine_len = 4 * coarse_len
    real_acc = None
    imag_acc = None
    for octant in range(octants):
        spread = jnp.repeat(extended[:, :, octant].astype(jnp.float32), 4, axis=-1)
        refined = jnp.zeros(spread.shape[:-1] + (fine_len,), jnp.float32)
        for stencil in range(taps_count):
            window = spread[..., 4 * stencil : 4 * stencil + fine_len]
            refined = refined + window * weights[stencil]
        cos_row = cosine[octant]
        sin_row = sine_part[octant]
        real_term = refined[0] * cos_row - refined[1] * sin_row
        imag_term = refined[0] * sin_row + refined[1] * cos_row
        if real_acc is None:
            real_acc = real_term
            imag_acc = imag_term
        else:
            real_acc = real_acc + real_term
            imag_acc = imag_acc + imag_term
    return jnp.stack([real_acc, imag_acc]).astype(jnp.bfloat16)


def local(children, present, interp, phase, trans, sources, trans_ids, list_len):
    present_mask = present.astype(jnp.bfloat16)[None, :, :, None, None, None]
    kept_children = children * present_mask
    cosine = jnp.cos(phase)
    sine_part = jnp.sin(phase)
    moved = two_step_exchange(kept_children, (("ang_0", "ang_1", "ang_2"), "ang_3"), (1, 0), 5, 1)
    extended = extended_2(moved, ((ANG, 5),), HW)
    fine_len = moved.shape[5] * 4
    first_index = lax.axis_index(ANG) * fine_len
    weights = lax.dynamic_slice_in_dim(interp, first_index, fine_len, 1)
    cosine_block = lax.dynamic_slice_in_dim(cosine, first_index, fine_len, 1)
    sine_block = lax.dynamic_slice_in_dim(sine_part, first_index, fine_len, 1)
    pattern = aggregate(extended, weights, cosine_block, sine_block, moved.shape[5])
    all_patterns = gathered_copies(pattern, "grp", 1)

    def one_slot(position, carried):
        real_sum, imag_sum = carried
        source_ids = lax.dynamic_index_in_dim(sources, position, 1, keepdims=False)
        operator_ids = lax.dynamic_index_in_dim(trans_ids, position, 1, keepdims=False)
        source_rows = jnp.take(all_patterns, source_ids, axis=1).astype(jnp.float32)
        operator_cols = jnp.take(trans, operator_ids, axis=1)[:, :, None, None, :]
        active = (position < list_len).astype(jnp.float32)[:, None, None, None]
        real_sum = real_sum + active * (
            operator_cols[0] * source_rows[0] - operator_cols[1] * source_rows[1]
        )
        imag_sum = imag_sum + active * (
            operator_cols[0] * source_rows[1] + operator_cols[1] * source_rows[0]
        )
        return (real_sum, imag_sum)

    zeros_start = jnp.zeros(pattern.shape[1:], jnp.float32)
    real_sum, imag_sum = lax.fori_loop(0, sources.shape[1], one_slot, (zeros_start, zeros_start))
    return jnp.stack([real_sum, imag_sum])


def solution(mesh):
    finer = Mesh(
        mesh.devices.reshape(mesh.shape["grp"], 2, 4, 4, 2),
        ("grp", "ang_0", "ang_1", "ang_2", "ang_3"),
    )
    placed = (
        P(None, GRP_ANG, None, None, None, None),
        P(GRP_ANG, None),
        P(),
        P(),
        P(None, None, ANG),
        P("grp", None),
        P("grp", None),
        P("grp"),
    )
    return jax.shard_map(
        local,
        mesh=finer,
        in_specs=placed,
        out_specs=P(None, "grp", None, None, ANG),
        check_vma=False,
    )
```

profile of v0, /device:TPU:0, one launch (start us, length us, event | category | flops | bytes accessed | tf_op | source)
XLA Modules:
  0.0 271.4 jit_solution(9242666889993987925)
XLA Ops:
  3.0 4.2 %all_to_all.15 = bf16[32,2,2,1,8,2,1,128]{7,4,6,5,3,2,0,1:T(8,128)(2,1)S(1)} all-to-all(bf16[32,2,2,1,8,2,1,128]{7,4,6,5,3,2,0,1:T(8,128)(2,1)S(1)} %copy.465), channel_id=1, replica_groups=mesh['grp'=2,'ang_0'=2,'ang_1'=4,'ang_2'=4,'ang_3'=2] {'ang_3'}, dimensions={1} | all-to-all | bytes 1048576 | tf_op jit(solution)/shard_map/all_to_all | solution.py:27
  8.0 10.7 %all-to-all-start.1 = ((bf16[32,2,2,1,8,2,1,128]{7,4,6,5,3,2,1,0:T(8,128)(2,1)}), bf16[32,2,2,1,8,2,1,128]{7,4,6,5,3,2,1,0:T(8,128)(2,1)S(1)}, u32[]{:S(2)}, u32[]{:S(2)}) async-start(bf16[32,2,2,1,8,2,1,128]{7,4,6,5,3,2,1,0:T(8,128)(2,1)} %copy.466), calls=%async_computation.1 | async-start | bytes 1048576 | tf_op jit(solution)/shard_map/all_to_all | solution.py:27
  19.6 12.6 %all-to-all-done.1 = bf16[32,2,2,1,8,2,1,128]{7,4,6,5,3,2,1,0:T(8,128)(2,1)S(1)} async-done(((bf16[32,2,2,1,8,2,1,128]{7,4,6,5,3,2,1,0:T(8,128)(2,1)}), bf16[32,2,2,1,8,2,1,128]{7,4,6,5,3,2,1,0:T(8,128)(2,1)S(1)}, u32[]{:S(2)}, u32[]{:S(2)}) %all-to-all-start.1) | async-done | bytes 524320 | tf_op jit(solution)/shard_map/all_to_all | solution.py:27
  32.5 7.6 %collective-permute-start.1 = (bf16[2,64,8,2,1,4]{5,2,3,0,1,4:T(8,128)(2,1)S(1)}, bf16[2,64,8,2,1,4]{5,2,3,0,1,4:T(8,128)(2,1)S(1)}, u32[]{:S(2)}, u32[]{:S(2)}) collective-permute-start(bf16[2,64,8,2,1,4]{5,2,3,0,1,4:T(8,128)(2,1)S(1)} %get-tuple-element.331), channel_id=1, source_target_pairs={{1,0},{2,1},{3,2},{4,3},{5,4},{6,5},{7,6},{8,7},{9,8},{10,9},{11,1... | collective-permute-start | bytes 49160 | tf_op jit(solution)/shard_map/ppermute | solution.py:46
  41.3 5.5 %collective-permute-done = bf16[2,64,8,2,1,4]{5,2,3,0,1,4:T(8,128)(2,1)S(1)} collective-permute-done((bf16[2,64,8,2,1,4]{5,2,3,0,1,4:T(8,128)(2,1)S(1)}, bf16[2,64,8,2,1,4]{5,2,3,0,1,4:T(8,128)(2,1)S(1)}, u32[]{:S(2)}, u32[]{:S(2)}) %collective-permute-start) | collective-permute-done | bytes 16416 | tf_op jit(solution)/shard_map/ppermute | solution.py:43
  47.4 2.5 slice_convert_fusion.7
  50.3 2.4 fusion.16
  52.7 2.4 copy.568
  59.7 2.3 copy.571
  62.1 2.3 copy.572
  68.3 2.4 fusion.17
  70.7 2.4 copy.576
  76.5 2.4 copy.579
  78.8 2.4 copy.580
  83.5 2.3 copy.583
  86.2 2.4 fusion.18
  92.1 2.4 copy.586
  96.8 2.4 copy.588
  101.3 2.3 copy.591
  104.1 2.4 fusion.19
  107.6 2.3 copy.593
  109.9 2.3 copy.594
  112.3 2.5 copy.595
  114.8 2.3 copy.596
  119.4 2.3 copy.599
  122.1 2.4 fusion.20
  125.6 2.3 copy.601
  130.3 2.4 copy.603
  132.7 2.4 copy.604
  137.4 2.3 copy.607
  140.1 2.4 fusion.21
  143.7 2.4 copy.609
  148.3 2.4 copy.611
  150.7 2.4 copy.612
  155.3 2.3 copy.615
  158.1 2.4 fusion.22
  161.6 2.3 copy.617
  163.9 2.4 copy.618
  166.3 2.4 copy.619
  176.0 2.4 fusion.23
  179.5 2.3 copy.625
  181.8 2.3 copy.626
  184.2 2.3 copy.627
  186.5 2.3 copy.628
  191.1 2.5 copy.631
  211.5 3.6 %all-to-all-start.2 = ((bf16[2,2,64,2,1,512]{5,2,3,1,4,0:T(8,128)(2,1)}), bf16[2,2,64,2,1,512]{5,2,3,1,4,0:T(8,128)(2,1)S(1)}, u32[]{:S(2)}, u32[]{:S(2)}) async-start(bf16[2,2,64,2,1,512]{5,2,3,1,4,0:T(8,128)(2,1)} %broadcast_in_dim.109), calls=%async_computation.2 | async-start | bytes 1048576 | tf_op jit(solution)/shard_map/all_to_all | solution.py:53
  215.2 6.5 %all-to-all-done.2 = bf16[2,2,64,2,1,512]{5,2,3,1,4,0:T(8,128)(2,1)S(1)} async-done(((bf16[2,2,64,2,1,512]{5,2,3,1,4,0:T(8,128)(2,1)}), bf16[2,2,64,2,1,512]{5,2,3,1,4,0:T(8,128)(2,1)S(1)}, u32[]{:S(2)}, u32[]{:S(2)}) %all-to-all-start.2) | async-done | bytes 524320 | tf_op jit(solution)/shard_map/all_to_all | solution.py:53
  221.8 47.5 %while.16 = (s32[]{:T(128)}, f32[64,2,1,512]{3,1,0,2:T(2,128)S(1)}, f32[64,2,1,512]{3,1,0,2:T(2,128)S(1)}, s32[64]{0:T(128)S(1)}, s32[64,8]{0,1:T(8,128)}, /*ind...) while((s32[]{:T(128)}, f32[64,2,1,512]{3,1,0,2:T(2,128)S(1)}, ...), condition=%wide.region_1.2_spmd.clone, body=%wide.region_0.1_spmd.clone.sunk | while | flops 1117059 | bytes 6302839 | solution.py:118
  (322 shorter events, 123.9 us)
Async XLA Ops:
  8.0 24.2 %all-to-all-start.1 = ((bf16[32,2,2,1,8,2,1,128]{7,4,6,5,3,2,1,0:T(8,128)(2,1)}), bf16[32,2,2,1,8,2,1,128]{7,4,6,5,3,2,1,0:T(8,128)(2,1)S(1)}, u32[]{:S(2)}, u32[]{:S(2)}) async-start(bf16[32,2,2,1,8,2,1,128]{7,4,6,5,3,2,1,0:T(8,128)(2,1)} %copy.466), calls=%async_computation.1 | async-start | bytes 1048576 | tf_op jit(solution)/shard_map/all_to_all | solution.py:27
  32.4 14.4 %collective-permute-start = (bf16[2,64,8,2,1,4]{5,2,3,0,1,4:T(8,128)(2,1)S(1)}, bf16[2,64,8,2,1,4]{5,2,3,0,1,4:T(8,128)(2,1)S(1)}, u32[]{:S(2)}, u32[]{:S(2)}) collective-permute-start(bf16[2,64,8,2,1,4]{5,2,3,0,1,4:T(8,128)(2,1)S(1)} %get-tuple-element.330), channel_id=1, source_target_pairs={{0,1},{1,2},{2,3},{3,4},{4,5},{5,6},{6,7},{7,8},{8,9},{9,10},{10,1... | collective-permute-start | bytes 49160 | tf_op jit(solution)/shard_map/ppermute | solution.py:43
  32.5 14.3 %collective-permute-start.1 = (bf16[2,64,8,2,1,4]{5,2,3,0,1,4:T(8,128)(2,1)S(1)}, bf16[2,64,8,2,1,4]{5,2,3,0,1,4:T(8,128)(2,1)S(1)}, u32[]{:S(2)}, u32[]{:S(2)}) collective-permute-start(bf16[2,64,8,2,1,4]{5,2,3,0,1,4:T(8,128)(2,1)S(1)} %get-tuple-element.331), channel_id=1, source_target_pairs={{1,0},{2,1},{3,2},{4,3},{5,4},{6,5},{7,6},{8,7},{9,8},{10,9},{11,1... | collective-permute-start | bytes 49160 | tf_op jit(solution)/shard_map/ppermute | solution.py:46
  82.3 3.5 %copy-start.66 = (f32[2,64,1,2,1,136]{5,2,3,0,1,4:T(1,128)S(1)}, f32[2,64,1,2,1,136]{5,2,3,0,1,4:T(1,128)}, u32[]{:S(2)}) copy-start(f32[2,64,1,2,1,136]{5,2,3,0,1,4:T(1,128)} %get-tuple-element.318) | copy-start | bytes 417796
  100.2 3.5 %copy-start.65 = (f32[2,64,1,2,1,136]{5,2,3,0,1,4:T(1,128)S(1)}, f32[2,64,1,2,1,136]{5,2,3,0,1,4:T(1,128)}, u32[]{:S(2)}) copy-start(f32[2,64,1,2,1,136]{5,2,3,0,1,4:T(1,128)} %get-tuple-element.317) | copy-start | bytes 417796
  118.3 3.5 %copy-start.64 = (f32[2,64,1,2,1,136]{5,2,3,0,1,4:T(1,128)S(1)}, f32[2,64,1,2,1,136]{5,2,3,0,1,4:T(1,128)}, u32[]{:S(2)}) copy-start(f32[2,64,1,2,1,136]{5,2,3,0,1,4:T(1,128)} %get-tuple-element.316) | copy-start | bytes 417796
  136.3 3.5 %copy-start.63 = (f32[2,64,1,2,1,136]{5,2,3,0,1,4:T(1,128)S(1)}, f32[2,64,1,2,1,136]{5,2,3,0,1,4:T(1,128)}, u32[]{:S(2)}) copy-start(f32[2,64,1,2,1,136]{5,2,3,0,1,4:T(1,128)} %get-tuple-element.315) | copy-start | bytes 417796
  154.2 3.5 %copy-start.62 = (f32[2,64,1,2,1,136]{5,2,3,0,1,4:T(1,128)S(1)}, f32[2,64,1,2,1,136]{5,2,3,0,1,4:T(1,128)}, u32[]{:S(2)}) copy-start(f32[2,64,1,2,1,136]{5,2,3,0,1,4:T(1,128)} %get-tuple-element.314) | copy-start | bytes 417796
  190.0 3.6 %copy-start.3 = (f32[2,64,2,1,512]{4,1,2,3,0:T(8,128)S(1)}, f32[2,64,2,1,512]{4,1,2,3,0:T(8,128)}, u32[]{:S(2)}) copy-start(f32[2,64,2,1,512]{4,1,2,3,0:T(8,128)} %copy.571) | copy-start | bytes 1572868
  190.0 3.6 %copy-start.4 = (f32[2,64,2,1,512]{4,1,2,3,0:T(8,128)S(1)}, f32[2,64,2,1,512]{4,1,2,3,0:T(8,128)}, u32[]{:S(2)}) copy-start(f32[2,64,2,1,512]{4,1,2,3,0:T(8,128)} %copy.572) | copy-start | bytes 1572868
  190.0 3.6 %copy-start.5 = (f32[2,64,2,1,512]{4,1,2,3,0:T(8,128)S(1)}, f32[2,64,2,1,512]{4,1,2,3,0:T(8,128)}, u32[]{:S(2)}) copy-start(f32[2,64,2,1,512]{4,1,2,3,0:T(8,128)} %copy.573) | copy-start | bytes 1572868
  191.1 2.5 copy-start
  191.1 2.5 copy-start.1
  191.1 2.5 copy-start.2
  193.6 2.2 copy-start.6
  193.6 2.2 copy-start.7
  193.6 2.2 copy-start.8
  193.6 2.2 copy-start.9
  193.6 2.2 copy-start.10
  193.7 2.2 copy-start.11
  193.7 2.3 copy-start.12
  193.7 2.4 copy-start.13
  196.1 1.7 copy-start.18
  196.1 1.8 copy-start.19
  196.1 2.0 copy-start.20
  196.1 2.1 copy-start.21
  198.3 1.7 copy-start.26
  198.3 1.8 copy-start.27
  198.3 2.0 copy-start.28
  198.3 2.1 copy-start.29
  200.4 1.7 copy-start.34
  200.4 1.8 copy-start.35
  200.4 2.0 copy-start.36
  200.4 2.1 copy-start.37
  202.6 1.7 copy-start.42
  202.6 1.8 copy-start.43
  202.6 2.0 copy-start.44
  202.6 2.1 copy-start.45
  204.7 1.7 copy-start.50
  204.7 1.8 copy-start.51
  204.7 2.0 copy-start.52
  204.7 2.1 copy-start.53
  206.9 1.7 copy-start.58
  206.9 1.8 copy-start.59
  206.9 2.0 copy-start.60
  206.9 2.1 copy-start.61
  211.5 10.2 %copy-start.68 = (s32[64]{0:T(128)S(1)}, s32[64]{0:T(128)}, u32[]{:S(2)}) copy-start(s32[64]{0:T(128)} %param.17) | copy-start | bytes 772
  211.5 10.2 %all-to-all-start.2 = ((bf16[2,2,64,2,1,512]{5,2,3,1,4,0:T(8,128)(2,1)}), bf16[2,2,64,2,1,512]{5,2,3,1,4,0:T(8,128)(2,1)S(1)}, u32[]{:S(2)}, u32[]{:S(2)}) async-start(bf16[2,2,64,2,1,512]{5,2,3,1,4,0:T(8,128)(2,1)} %broadcast_in_dim.109), calls=%async_computation.2 | async-start | bytes 1048576 | tf_op jit(solution)/shard_map/all_to_all | solution.py:53
  (25 other events, 31.8 us)
where the time goes:
time: 277 us; the launch traced here: 271 us
  local copies, waits for them, and re-layouts  191 us (69%)
  other arithmetic  28.1 us (10%)
  waiting for transfers between devices  24.6 us (9%)
  starting transfers between devices  22 us (8%)
  blocking collectives  4.15 us (1%)
    unnamed x202, local copies, waits for them, and re-layouts  131 us
    slice x8, local copies, waits for them, and re-layouts, aggregate(): window = spread[..., 4 * stencil:4 * stencil + fine_len]  19.2 us
    gather x8, local copies, waits for them, and re-layouts, one_slot(): operator_cols = jnp.take(trans, operator_ids, axis=1)[:, :, None, None, :]  17.3 us
    all_to_all x1, waiting for transfers between devices, exchange_in_order(): lax.all_to_all(parts, axes[k], split_axis=k, concat_axis=k, tiled=True)  12.6 us
    all_to_all x1, starting transfers between devices, exchange_in_order(): lax.all_to_all(parts, axes[k], split_axis=k, concat_axis=k, tiled=True)  10.7 us
    gather x8, local copies, waits for them, and re-layouts, one_slot(): source_rows = jnp.take(all_patterns, source_ids, axis=1).astype(jnp.float32)  8.94 us
    ppermute x1, starting transfers between devices, extended_2(): lax.ppermute(lax.slice_in_dim(block, 0, width, axis=dim), axis, backward)  7.61 us
    all_to_all x1, waiting for transfers between devices, sent_to_all(): lax.all_to_all(jnp.broadcast_to(value[None], (length, *value.shape)), axi...  6.54 us
  transfers between devices with their start and end apart: 4, of which 3 were waited for; matrix products, arithmetic and copies ran while one was open for 1% of the time, Pallas kernels for 0%

commit v1 on v0

v1 whole, which is shorter than its diff:
```python
import functools

import jax
import jax.numpy as jnp
from jax import lax
from jax.experimental import pallas as pl
from jax.experimental.pallas import tpu as pltpu
from jax.sharding import PartitionSpec as P

HW = 4
LANES = 128
F32 = jnp.float32
BF16 = jnp.bfloat16

SIN_TERMS = (-0.1666666567325592, 0.008333242498338223, -0.00019822783360723406, 2.634888232933008e-06)
COS_TERMS = (0.0416666679084301, -0.0013888812391087413, 2.4786117137409747e-05, -2.6547101583673793e-07)


def horner(terms, z):
    total = jnp.full_like(z, terms[-1])
    for term in terms[-2::-1]:
        total = total * z + term
    return total


def sin_cos(angle):
    half = angle * 0.5
    z = half * half
    sin_half = half + (half * z) * horner(SIN_TERMS, z)
    cos_half = (1.0 - 0.5 * z) + (z * z) * horner(COS_TERMS, z)
    twice = sin_half + sin_half
    return twice * cos_half, 1.0 - twice * sin_half


def row_sums(rows):
    place = lax.broadcasted_iota(jnp.int32, rows[0].shape, 0)
    for distance in (1, 2, 4):
        first = (place & distance) == 0
        rows = [
            jnp.where(first, a, b) + pltpu.roll(jnp.where(first, b, a), distance, 0)
            for a, b in zip(rows[0::2], rows[1::2])
        ]
    return rows[0]


def aggregate_kernel(blocks, total, present_ref, children_ref, interp_ref, phase_ref, out_ref):
    step = pl.program_id(0)
    lane = lax.broadcasted_iota(jnp.int32, (8, LANES), 1)
    row = lax.broadcasted_iota(jnp.int32, (8, LANES), 0)
    kept = jnp.zeros((8, LANES), F32)
    for octant in range(8):
        kept = jnp.where(row == octant, present_ref[0, octant].astype(F32), kept)
    kept = jnp.concatenate([kept] * 4, axis=0)
    lane32 = lax.broadcasted_iota(jnp.int32, (32, LANES), 1)
    fine_lane = lax.broadcasted_iota(jnp.int32, (8, 4 * LANES), 1)
    bits = [((fine_lane // 4) & d) != 0 for d in (1, 2, 4)]
    row16 = lax.broadcasted_iota(jnp.int32, (16, LANES), 0)
    lane16 = lax.broadcasted_iota(jnp.int32, (16, LANES), 1) // 4
    bands = []
    for i in range(3):
        tap = row16 + 16 * i - lane16
        bands.append(jnp.where((tap >= 0) & (tap < 8), 1.0, 0.0).astype(BF16))
    nothing = jnp.zeros((16, LANES), BF16)

    for i in range(blocks):
        a = step * blocks + i

        def coarse(index):
            at = pl.multiple_of(index * LANES, LANES)
            return children_ref[:, pl.ds(at, LANES)].astype(F32) * kept

        before = coarse(lax.rem(a + total - 1, total))
        here = coarse(a)
        after = coarse(lax.rem(a + 1, total))
        windows = (
            jnp.where(lane32 < HW, pltpu.roll(before, HW, 1), pltpu.roll(here, HW, 1)).astype(BF16),
            jnp.where(lane32 < 64 + HW, pltpu.roll(here, 64 + HW, 1), pltpu.roll(after, 64 + HW, 1)).astype(BF16),
        )
        fine = pl.ds(4 * LANES * i, 4 * LANES)
        turned = interp_ref[:, fine]
        for bit, distance in zip(bits, (1, 2, 4)):
            turned = jnp.where(bit, pltpu.roll(turned, distance, 0), turned)
        turned = jnp.concatenate([turned, turned], axis=0)
        high = turned.astype(BF16)
        low = (turned - high.astype(F32)).astype(BF16)
        sine, cosine = sin_cos(phase_ref[:, fine])
        real = [None] * 8
        imag = [None] * 8
        for half in range(2):
            weights = []
            for part in (high, low):
                left = part[:, (2 * half) * LANES : (2 * half + 1) * LANES]
                right = part[:, (2 * half + 1) * LANES : (2 * half + 2) * LANES]
                weights.append(
                    jnp.concatenate(
                        [
                            jnp.concatenate([left * b for b in bands] + [nothing] * 5, axis=0),
                            jnp.concatenate([nothing] * 2 + [right * b for b in bands] + [nothing] * 3, axis=0),
                        ],
                        axis=1,
                    )
                )
            refined = jnp.dot(
                jnp.concatenate([windows[half], windows[half]], axis=1),
                jnp.concatenate(weights, axis=0),
                preferred_element_type=F32,
            )
            for tile in range(2):
                at = (2 * half + tile) * LANES
                cos_tile = cosine[:, at : at + LANES]
                sin_tile = sine[:, at : at + LANES]
                for pol in range(2):
                    re = refined[8 * pol : 8 * pol + 8, tile * LANES : (tile + 1) * LANES]
                    im = refined[16 + 8 * pol : 24 + 8 * pol, tile * LANES : (tile + 1) * LANES]
                    spot = 2 * (2 * half + tile) + pol
                    real[spot] = re * cos_tile - im * sin_tile
                    imag[spot] = re * sin_tile + im * cos_tile
        pattern = jnp.concatenate([row_sums(real), row_sums(imag)], axis=0).astype(BF16)
        for group in range(out_ref.shape[0]):
            out_ref[group, i] = pattern


def translate_kernel(
    receivers, sources_ref, ids_ref, used_ref, pattern_ref, trans_ref, out_ref, unpacked
):
    step = pl.program_id(0)
    clusters = pattern_ref.shape[0]
    slots = sources_ref.shape[0]

    @pl.when(step == 0)
    def _():
        def unpack(c, carry):
            unpacked[c] = pattern_ref[c].astype(F32)
            return carry

        lax.fori_loop(0, clusters, unpack, 0, unroll=8)
        unpacked[clusters] = jnp.zeros((16, LANES), F32)

    row = lax.broadcasted_iota(jnp.int32, (8, LANES), 0)
    even = (row & 1) == 0
    order = 2 * (row & 3) + (row >> 2)

    def receive(c, carry):
        receiver = step * receivers + c
        used = used_ref[receiver]
        real = jnp.zeros((8, LANES), F32)
        imag = jnp.zeros((8, LANES), F32)
        for slot in range(slots):
            source = jnp.where(slot < used, sources_ref[slot, receiver], clusters)
            operator = trans_ref[ids_ref[slot, receiver]]
            values = unpacked[source]
            re, im = values[:8], values[8:]
            t_re = jnp.where(even, operator, pltpu.roll(operator, 1, 0))
            t_im = jnp.where(even, pltpu.roll(operator, 7, 0), operator)
            real = real + (t_re * re - t_im * im)
            imag = imag + (t_re * im + t_im * re)
        out_ref[0, c] = jnp.take_along_axis(real, order, axis=0)
        out_ref[1, c] = jnp.take_along_axis(imag, order, axis=0)
        return carry

    lax.fori_loop(0, receivers, receive, 0, unroll=4)


def aggregate(children, present, interp, phase, copies):
    rows, coarse_len = children.shape
    fine_len = interp.shape[1]
    total = coarse_len // LANES
    steps = 8
    blocks = total // steps
    return pl.pallas_call(
        functools.partial(aggregate_kernel, blocks, total),
        grid=(steps,),
        in_specs=[
            pl.BlockSpec(memory_space=pltpu.SMEM),
            pl.BlockSpec((rows, coarse_len), lambda s: (0, 0)),
            pl.BlockSpec((8, fine_len // steps), lambda s: (0, s)),
            pl.BlockSpec((8, fine_len // steps), lambda s: (0, s)),
        ],
        out_specs=pl.BlockSpec((copies, blocks, 16, LANES), lambda s: (0, s, 0, 0)),
        out_shape=jax.ShapeDtypeStruct((copies, total, 16, LANES), BF16),
        name="aggregate",
    )(present, children, interp, phase)


def translate(sources, ids, used, pattern, trans):
    slots, local = sources.shape
    clusters = pattern.shape[0]
    steps = 4
    receivers = local // steps
    return pl.pallas_call(
        functools.partial(translate_kernel, receivers),
        grid=(steps,),
        in_specs=[
            pl.BlockSpec(memory_space=pltpu.SMEM),
            pl.BlockSpec(memory_space=pltpu.SMEM),
            pl.BlockSpec(memory_space=pltpu.SMEM),
            pl.BlockSpec((clusters, 16, LANES), lambda s: (0, 0, 0)),
            pl.BlockSpec(trans.shape, lambda s: (0, 0, 0)),
        ],
        out_specs=pl.BlockSpec((2, receivers, 8, LANES), lambda s: (0, s, 0, 0)),
        out_shape=jax.ShapeDtypeStruct((2, local, 8, LANES), F32),
        scratch_shapes=[pltpu.VMEM((clusters + 1, 16, LANES), F32)],
        name="translate",
    )(sources, ids, used, pattern, trans)


def local(children, present, interp, phase, trans, sources, trans_ids, list_len):
    groups = lax.axis_size("grp")
    rows = jnp.transpose(children[:, 0, :, :, 0], (0, 2, 1, 3)).reshape(32, -1)
    pattern = aggregate(rows, present, interp, phase, groups)
    pattern = lax.all_to_all(
        pattern.reshape(-1, 16, LANES), ("grp", "ang"), 0, 0, tiled=True
    )
    kinds = trans.shape[1]
    operators = jnp.transpose(
        jnp.transpose(trans, (1, 0, 2)).reshape(kinds, 2, 4, LANES), (0, 2, 1, 3)
    ).reshape(kinds, 8, LANES)
    out = translate(sources.T, trans_ids.T, list_len, pattern, operators)
    return out.reshape(2, -1, 2, 1, 4 * LANES)


def solution(mesh):
    placed = (
        P(None, ("grp", "ang"), None, None, None, None),
        P(("grp", "ang"), None),
        P(),
        P(),
        P(None, None, "ang"),
        P("grp", None),
        P("grp", None),
        P("grp"),
    )
    return jax.shard_map(
        local,
        mesh=mesh,
        in_specs=placed,
        out_specs=P(None, "grp", None, None, "ang"),
        check_vma=False,
    )
```

time: 277 us -> 39.4 us (0.14)
  the two profiles are of different devices: /device:TPU:0 before, /device:TPU:1 now
where the time goes in v1:
time: 39.4 us; the launch traced here: 39 us
  blocking collectives  25.1 us (64%)
  Pallas kernels  11.7 us (30%)
  local copies, waits for them, and re-layouts  2.13 us (5%)
    all_to_all x1, blocking collectives, local(): lax.all_to_all(pattern.reshape(-1, 16, LANES), ('grp', 'ang'), 0, 0, tile...  25.1 us
    pallas_call x1, Pallas kernels, aggregate(): pl.pallas_call(functools.partial(aggregate_kernel, blocks, total), grid=(...  7.56 us
    pallas_call x1, Pallas kernels, translate(): pl.pallas_call(functools.partial(translate_kernel, receivers), grid=(step...  4.17 us
    transpose x1, local copies, waits for them, and re-layouts, local(): rows = jnp.transpose(children[:, 0, :, :, 0], (0, 2, 1, 3)).reshape(32, -1)  2.13 us

profile of v1, /device:TPU:1, one launch (start us, length us, event | category | flops | bytes accessed | tf_op | source)
XLA Modules:
  0.0 39.0 jit_solution(1208791752589888965)
XLA Ops:
  0.0 2.1 %copy.9 = bf16[2,2,8,8192]{3,2,1,0:T(8,128)(2,1)} copy(bf16[2,2,8,8192]{3,1,2,0:T(2,128)(2,1)} %bitcast.18) | data formatting | bytes 1048576 | tf_op jit(solution)/shard_map/transpose | solution.py:209
  2.1 7.6 %aggregate.1 = bf16[2,64,16,128]{3,2,1,0:T(8,128)(2,1)} custom-call(s32[1,8]{1,0:T(1,128)} %present_ref.1, bf16[32,8192]{1,0:T(8,128)(2,1)} %bitcast.16, f32[8,32768]{1,0:T(8,128)} %interp_ref.1, f32[8,32768]{1,0:T(8,128)} %phase_ref.1), custom_call_target="tpu_custom_call" | custom-call | tf_op jit(solution)/shard_map/aggregate/pallas_call | solution.py:170
  9.7 25.1 %all_to_all.5.pattern_ref = bf16[128,16,128]{2,1,0:T(8,128)(2,1)} all-to-all(bf16[128,16,128]{2,1,0:T(8,128)(2,1)} %bitcast.15), channel_id=1, replica_groups=mesh['grp'=2,'ang'=64] {'grp','ang'}, dimensions={0} | all-to-all | bytes 1048576 | tf_op jit(solution)/shard_map/all_to_all | solution.py:211
  34.8 4.2 %translate.1 = f32[2,64,8,128]{3,2,1,0:T(8,128)} custom-call(s32[8,64]{1,0:T(8,128)} %bitcast.19, s32[8,64]{1,0:T(8,128)} %bitcast.20, s32[64]{0:T(128)} %used_ref.1, bf16[128,16,128]{2,1,0:T(8,128)(2,1)} %all_to_all.5.pattern_ref, f32[316,8,128]{2,1,0:T(8,128)} %bitcast.17), custom_call_target="tpu_custom_call" | custom-call | tf_op jit(solution)/shard_map/translate/pallas_call | solution.py:190

commit v2 on v1

v2 whole, which is shorter than its diff:
```python
import functools

import jax
import jax.numpy as jnp
from jax import lax
from jax.experimental import pallas as pl
from jax.experimental.pallas import tpu as pltpu
from jax.sharding import PartitionSpec as P

HW = 4
LANES = 128
CHUNK = 32
BATCH = 8
F32 = jnp.float32
BF16 = jnp.bfloat16
ROOT = 2.0**0.5

SIN_TERMS = tuple(
    ROOT * v * 0.5 ** (2 * i + 1)
    for i, v in enumerate((1.0, -0.1666666567325592, 0.008333242498338223, -0.00019822783360723406, 2.634888232933008e-06))
)
COS_TERMS = tuple(
    ROOT * v * 0.25**i
    for i, v in enumerate(
        (1.0, -0.5, 0.0416666679084301, -0.0013888812391087413, 2.4786117137409747e-05, -2.6547101583673793e-07)
    )
)


def horner(terms, z):
    total = z * terms[-1] + terms[-2]
    for term in terms[-3::-1]:
        total = total * z + term
    return total


def sin_cos(angle):
    z = angle * angle
    sin_half = angle * horner(SIN_TERMS, z)
    cos_half = horner(COS_TERMS, z)
    return sin_half * cos_half, 1.0 - sin_half * sin_half


def row_sums(rows):
    place = lax.broadcasted_iota(jnp.int32, rows[0].shape, 0)
    for distance in (1, 2, 4):
        first = (place & distance) == 0
        rows = [
            jnp.where(first, a, b) + pltpu.roll(jnp.where(first, b, a), distance, 0)
            for a, b in zip(rows[0::2], rows[1::2])
        ]
    return rows[0]


def aggregate_kernel(
    present_ref, children_ref, interp_ref, phase_ref, out_ref,
    stored, spread, weights_in, phase_in, patterns, flags, child_sem, flag_sem, weight_sem, phase_sem, out_sem,
):
    groups, total = out_ref.shape[:2]
    chunks = total // CHUNK
    span = 4 * LANES * CHUNK
    octants = 8
    parts = 2

    def weight_copy(c):
        at = pl.ds(pl.multiple_of(c * span, span), span)
        return pltpu.make_async_copy(interp_ref.at[:, at], weights_in.at[:, at], weight_sem.at[c])

    def phase_copy(c):
        at = pl.ds(pl.multiple_of(c * span, span), span)
        return pltpu.make_async_copy(phase_ref.at[:, at], phase_in.at[:, at], phase_sem.at[c])

    def out_copy(c, g):
        at = pl.ds(c * CHUNK, CHUNK)
        return pltpu.make_async_copy(patterns.at[at], out_ref.at[g, at], out_sem.at[c, g])

    child_copy = pltpu.make_async_copy(children_ref, stored, child_sem)
    child_copy.start()
    flag_copy = pltpu.make_async_copy(present_ref, flags, flag_sem)
    flag_copy.start()
    for c in range(chunks):
        weight_copy(c).start()
        phase_copy(c).start()
    flag_copy.wait()
    child_copy.wait()

    per = 2 * total
    for octant in range(octants):
        flag = flags[0, octant].astype(F32)
        for part in range(parts):

            def unpack(m, carry, flag=flag, octant=octant, part=part):
                at = pl.multiple_of((part * octants + octant) * per + 16 * m, 16)
                rows = stored[pl.ds(at, 16), :].astype(F32) * flag
                to = (part * per + 16 * m) * octants + octant
                spread[pl.ds(to, 8, stride=octants), :] = rows[:8]
                spread[pl.ds(to + 8 * octants, 8, stride=octants), :] = rows[8:]
                return carry

            lax.fori_loop(0, per // 16, unpack, 0, unroll=True)

    lane = lax.broadcasted_iota(jnp.int32, (8, LANES), 1)
    row = lax.broadcasted_iota(jnp.int32, (8, LANES), 0)
    turn = (row - lane // 4) & 7
    row16 = lax.broadcasted_iota(jnp.int32, (16, LANES), 0)
    lane16 = lax.broadcasted_iota(jnp.int32, (16, LANES), 1) // 4
    bands = []
    for i in range(3):
        tap = row16 + 16 * i - lane16
        bands.append(jnp.where((tap >= 0) & (tap < 8), 1.0, 0.0).astype(BF16))
    nothing = jnp.zeros((16, LANES), BF16)

    def coarse(index):
        return [
            spread[pl.ds(pl.multiple_of((part * per + 2 * index + pol) * octants, 8), 8), :]
            for part in range(parts)
            for pol in range(2)
        ]

    def chunk(c, carry):
        weight_copy(c).wait()
        phase_copy(c).wait()
        near, far = [], []
        for i in range(-1, CHUNK + 1):
            values = coarse(lax.rem(c * CHUNK + i + total, total))
            near.append([pltpu.roll(v, HW, 1) for v in values] if i < CHUNK else None)
            far.append([pltpu.roll(v, 64 + HW, 1) for v in values] if i >= 0 else None)
        for i in range(CHUNK):
            windows = (
                jnp.concatenate([jnp.where(lane < HW, b, h) for b, h in zip(near[i], near[i + 1])], axis=0).astype(BF16),
                jnp.concatenate([jnp.where(lane < 64 + HW, h, a) for h, a in zip(far[i + 1], far[i + 2])], axis=0).astype(BF16),
            )
            base = pl.multiple_of(c * span, span) + 4 * LANES * i
            real = [None] * 8
            imag = [None] * 8
            for half in range(2):
                high, low = [], []
                for tile in range(2):
                    at = pl.ds(base + (2 * half + tile) * LANES, LANES)
                    turned = jnp.take_along_axis(weights_in[:, at], turn, axis=0, mode="promise_in_bounds")
                    turned = jnp.concatenate([turned, turned], axis=0)
                    top = turned.astype(BF16)
                    high.append(top)
                    low.append((turned - top.astype(F32)).astype(BF16))
                weights = [
                    jnp.concatenate(
                        [
                            jnp.concatenate([left * b for b in bands] + [nothing] * 5, axis=0),
                            jnp.concatenate([nothing] * 2 + [right * b for b in bands] + [nothing] * 3, axis=0),
                        ],
                        axis=1,
                    )
                    for left, right in (high, low)
                ]
                refined = jnp.dot(
                    jnp.concatenate([windows[half], windows[half]], axis=1),
                    jnp.concatenate(weights, axis=0),
                    preferred_element_type=F32,
                )
                for tile in range(2):
                    at = pl.ds(base + (2 * half + tile) * LANES, LANES)
                    sin_tile, cos_tile = sin_cos(phase_in[:, at])
                    for pol in range(2):
                        re = refined[8 * pol : 8 * pol + 8, tile * LANES : (tile + 1) * LANES]
                        im = refined[16 + 8 * pol : 24 + 8 * pol, tile * LANES : (tile + 1) * LANES]
                        spot = 2 * (2 * half + tile) + pol
                        real[spot] = re * cos_tile - im * sin_tile
                        imag[spot] = re * sin_tile + im * cos_tile
            patterns[c * CHUNK + i] = jnp.concatenate([row_sums(real), row_sums(imag)], axis=0).astype(BF16)
        for g in range(groups):
            out_copy(c, g).start()
        return carry

    lax.fori_loop(0, chunks, chunk, 0)
    for c in range(chunks):
        for g in range(groups):
            out_copy(c, g).wait()


def aggregate(children, present, interp, phase, groups):
    total = children.shape[0] // 32
    chunks = total // CHUNK
    anywhere = pl.BlockSpec(memory_space=pl.ANY)
    return pl.pallas_call(
        aggregate_kernel,
        in_specs=[anywhere, anywhere, anywhere, anywhere],
        out_specs=anywhere,
        out_shape=jax.ShapeDtypeStruct((groups, total, 16, LANES), BF16),
        scratch_shapes=[
            pltpu.VMEM(children.shape, BF16),
            pltpu.VMEM(children.shape, F32),
            pltpu.VMEM(interp.shape, F32),
            pltpu.VMEM(phase.shape, F32),
            pltpu.VMEM((total, 16, LANES), BF16),
            pltpu.SMEM(present.shape, jnp.int32),
            pltpu.SemaphoreType.DMA,
            pltpu.SemaphoreType.DMA,
            pltpu.SemaphoreType.DMA((chunks,)),
            pltpu.SemaphoreType.DMA((chunks,)),
            pltpu.SemaphoreType.DMA((chunks, groups)),
        ],
        name="aggregate",
    )(present, children, interp, phase)


def aggregate_local(children, present, interp, phase, groups=2):
    total = children.shape[5] // LANES
    rows = jnp.transpose(children.reshape(2, 8, 2, total, LANES), (0, 1, 3, 2, 4)).reshape(-1, LANES)
    return aggregate(rows, present, interp, phase, groups)


def translate_kernel(
    sources_ref, ids_ref, used_ref, pattern_ref, trans_ref, out_ref, places, table, unpacked, received, table_sem, out_sem
):
    slots, receivers = sources_ref.shape
    clusters = pattern_ref.shape[0] // 16
    batches = receivers // BATCH

    def out_copy(b):
        at = pl.ds(b * BATCH, BATCH)
        return pltpu.make_async_copy(received.at[:, at], out_ref.at[:, at], out_sem.at[b])

    slot_row = lax.broadcasted_iota(jnp.int32, (slots, receivers), 0)
    places[:slots, :] = jnp.where(slot_row < used_ref[...], sources_ref[...], clusters) * 16
    places[slots:, :] = ids_ref[...] * 8
    table_copy = pltpu.make_async_copy(places, table, table_sem)
    table_copy.start()

    def unpack(c, carry):
        at = pl.ds(pl.multiple_of(16 * c, 16), 16)
        unpacked[at, :] = pattern_ref[at, :].astype(F32)
        return carry

    lax.fori_loop(0, clusters, unpack, 0, unroll=8)
    unpacked[pl.ds(16 * clusters, 16), :] = jnp.zeros((16, LANES), F32)
    row = lax.broadcasted_iota(jnp.int32, (8, LANES), 0)
    even = (row & 1) == 0
    order = 2 * (row & 3) + (row >> 2)
    table_copy.wait()

    for receiver in range(receivers):
        real = imag = None
        for slot in range(slots):
            source = pl.multiple_of(table[slot, receiver], 16)
            operator = trans_ref[pl.ds(pl.multiple_of(table[slots + slot, receiver], 8), 8), :]
            re = unpacked[pl.ds(source, 8), :]
            im = unpacked[pl.ds(source + 8, 8), :]
            t_re = jnp.where(even, operator, pltpu.roll(operator, 1, 0))
            t_im = jnp.where(even, pltpu.roll(operator, 7, 0), operator)
            new_re = t_re * re - t_im * im
            new_im = t_re * im + t_im * re
            real = new_re if real is None else real + new_re
            imag = new_im if imag is None else imag + new_im
        received[0, receiver] = jnp.take_along_axis(real, order, axis=0, mode="promise_in_bounds")
        received[1, receiver] = jnp.take_along_axis(imag, order, axis=0, mode="promise_in_bounds")
        if (receiver + 1) % BATCH == 0:
            out_copy(receiver // BATCH).start()
    for b in range(batches):
        out_copy(b).wait()


def translate_local(sources, trans_ids, list_len, pattern, trans):
    kinds = trans.shape[1]
    receivers, slots = sources.shape
    clusters = pattern.shape[0]
    operators = jnp.transpose(
        jnp.transpose(trans, (1, 0, 2)).reshape(kinds, 2, 4, LANES), (0, 2, 1, 3)
    ).reshape(kinds * 8, LANES)
    inside = pl.BlockSpec(memory_space=pltpu.VMEM)
    out = pl.pallas_call(
        translate_kernel,
        in_specs=[inside] * 5,
        out_specs=pl.BlockSpec(memory_space=pl.ANY),
        out_shape=jax.ShapeDtypeStruct((2, receivers, 8, LANES), F32),
        scratch_shapes=[
            pltpu.VMEM((2 * slots, receivers), jnp.int32),
            pltpu.SMEM((2 * slots, receivers), jnp.int32),
            pltpu.VMEM((16 * (clusters + 1), LANES), F32),
            pltpu.VMEM((2, receivers, 8, LANES), F32),
            pltpu.SemaphoreType.DMA,
            pltpu.SemaphoreType.DMA((receivers // BATCH,)),
        ],
        compiler_params=pltpu.CompilerParams(vmem_limit_bytes=16 * 2**20),
        name="translate",
    )(sources.T, trans_ids.T, list_len.reshape(1, -1), pattern.reshape(-1, LANES), operators)
    return out.reshape(2, -1, 2, 1, 4 * LANES)


def local(children, present, interp, phase, trans, sources, trans_ids, list_len):
    pattern = aggregate_local(children, present, interp, phase, lax.axis_size("grp"))
    pattern = lax.all_to_all(
        pattern.reshape(-1, 16, LANES), ("grp", "ang"), 0, 0, tiled=True
    )
    return translate_local(sources, trans_ids, list_len, pattern, trans)


def solution(mesh):
    placed = (
        P(None, ("grp", "ang"), None, None, None, None),
        P(("grp", "ang"), None),
        P(),
        P(),
        P(None, None, "ang"),
        P("grp", None),
        P("grp", None),
        P("grp"),
    )
    return jax.shard_map(
        local,
        mesh=mesh,
        in_specs=placed,
        out_specs=P(None, "grp", None, None, "ang"),
        check_vma=False,
    )
```

time: 39.4 us -> 33.3 us (0.85)
  Pallas kernels: 11.7 us -> 8.06 us
  local copies, waits for them, and re-layouts: 2.13 us -> 0.02 us
    pallas_call x2, Pallas kernels: 11.7 us -> 8.06 us  [the longest x1 5.84 us: aggregate(): pl.pallas_call(aggregate_kernel, in_specs=[anywhere, anywhere, anywhere,...]
    transpose x1 -> x0, local copies, waits for them, and re-layouts: 2.13 us -> none  [local(): rows = jnp.transpose(children[:, 0, :, :, 0], (0, 2, 1, 3)).reshape(32, -1)]
where the time goes in v2:
time: 33.3 us; the launch traced here: 33.2 us
  blocking collectives  25.1 us (75%)
  Pallas kernels  8.06 us (24%)
    all_to_all x1, blocking collectives, local(): lax.all_to_all(pattern.reshape(-1, 16, LANES), ('grp', 'ang'), 0, 0, tile...  25.1 us
    pallas_call x1, Pallas kernels, aggregate(): pl.pallas_call(aggregate_kernel, in_specs=[anywhere, anywhere, anywhere,...  5.84 us
    pallas_call x1, Pallas kernels, translate_local(): pl.pallas_call(translate_kernel, in_specs=[inside] * 5, out_specs=pl.Bloc...  2.22 us

profile of v2, /device:TPU:1, one launch (start us, length us, event | category | flops | bytes accessed | tf_op | source)
XLA Modules:
  0.0 33.2 jit_solution(17042024816093489292)
XLA Ops:
  0.0 0.0 copy-start
  0.0 0.0 copy-start.1
  0.0 0.0 copy-start.2
  0.0 0.0 copy-start.3
  0.0 5.8 %aggregate.1 = bf16[2,64,16,128]{3,2,1,0:T(8,128)(2,1)} custom-call(s32[1,8]{1,0:T(1,128)} %present_ref.1, bf16[2048,128]{1,0:T(8,128)(2,1)} %bitcast.24, f32[8,32768]{1,0:T(8,128)} %interp_ref.1, f32[8,32768]{1,0:T(8,128)} %phase_ref.1), custom_call_target="tpu_custom_call" | custom-call | tf_op jit(solution)/shard_map/aggregate/pallas_call | solution.py:184
  5.9 25.1 %all_to_all.5 = bf16[128,16,128]{2,1,0:T(8,128)(2,1)S(1)} all-to-all(bf16[128,16,128]{2,1,0:T(8,128)(2,1)} %bitcast.23), channel_id=1, replica_groups=mesh['grp'=2,'ang'=64] {'grp','ang'}, dimensions={0} | all-to-all | bytes 1048576 | tf_op jit(solution)/shard_map/all_to_all | solution.py:291
  30.9 0.0 copy-done
  30.9 0.0 copy-done.1
  30.9 0.0 copy-done.2
  30.9 0.0 copy-done.3
  30.9 2.2 %translate.1 = f32[2,64,8,128]{3,2,1,0:T(8,128)} custom-call(s32[8,64]{1,0:T(8,128)S(1)} %bitcast.20, s32[8,64]{1,0:T(8,128)S(1)} %bitcast.21, s32[1,64]{1,0:T(1,128)S(1)} %bitcast.22, bf16[2048,128]{1,0:T(8,128)(2,1)S(1)} %bitcast.18, f32[2528,128]{1,0:T(8,128)S(1)} %bitcast.19), custom_call_target="tpu_custom_call" | custom-call | tf_op jit(solution)/shard_map/translate/pallas_call | solution.py:270
Async XLA Ops:
  0.0 30.9 %copy-start = (f32[2,316,512]{2,0,1:T(2,128)S(1)}, f32[2,316,512]{2,0,1:T(2,128)}, u32[]{:S(2)}) copy-start(f32[2,316,512]{2,0,1:T(2,128)} %param.12) | copy-start | bytes 3883012
  0.0 30.9 %copy-start.1 = (s32[64,8]{0,1:T(8,128)S(1)}, s32[64,8]{0,1:T(8,128)}, u32[]{:S(2)}) copy-start(s32[64,8]{0,1:T(8,128)} %param.13) | copy-start | bytes 6148
  0.0 30.9 %copy-start.2 = (s32[64,8]{0,1:T(8,128)S(1)}, s32[64,8]{0,1:T(8,128)}, u32[]{:S(2)}) copy-start(s32[64,8]{0,1:T(8,128)} %param.14) | copy-start | bytes 6148
  0.0 30.9 %copy-start.3 = (s32[64]{0:T(128)S(1)}, s32[64]{0:T(128)}, u32[]{:S(2)}) copy-start(s32[64]{0:T(128)} %param.15) | copy-start | bytes 772

commit v3 on v2

--- a/solution.py
+++ b/solution.py
@@ -10,6 +10,7 @@
 HW = 4
 LANES = 128
 CHUNK = 32
+LIMIT = 57000
 BATCH = 8
 F32 = jnp.float32
 BF16 = jnp.bfloat16
@@ -54,13 +55,14 @@
 
 def aggregate_kernel(
     present_ref, children_ref, interp_ref, phase_ref, out_ref,
-    stored, spread, weights_in, phase_in, patterns, flags, child_sem, flag_sem, weight_sem, phase_sem, out_sem,
+    stored, spread, weights_in, phase_in, flags, child_sem, flag_sem, weight_sem, phase_sem,
 ):
     groups, total = out_ref.shape[:2]
     chunks = total // CHUNK
     span = 4 * LANES * CHUNK
     octants = 8
     parts = 2
+    per = 2 * total
 
     def weight_copy(c):
         at = pl.ds(pl.multiple_of(c * span, span), span)
@@ -70,24 +72,23 @@
         at = pl.ds(pl.multiple_of(c * span, span), span)
         return pltpu.make_async_copy(phase_ref.at[:, at], phase_in.at[:, at], phase_sem.at[c])
 
-    def out_copy(c, g):
-        at = pl.ds(c * CHUNK, CHUNK)
-        return pltpu.make_async_copy(patterns.at[at], out_ref.at[g, at], out_sem.at[c, g])
-
-    child_copy = pltpu.make_async_copy(children_ref, stored, child_sem)
-    child_copy.start()
+    def child_copy(k):
+        at = pl.ds(k * per, per)
+        return pltpu.make_async_copy(children_ref.at[at], stored.at[at], child_sem.at[k])
+
     flag_copy = pltpu.make_async_copy(present_ref, flags, flag_sem)
     flag_copy.start()
+    for k in range(parts * octants):
+        child_copy(k).start()
     for c in range(chunks):
         weight_copy(c).start()
         phase_copy(c).start()
     flag_copy.wait()
-    child_copy.wait()
-
-    per = 2 * total
+
     for octant in range(octants):
         flag = flags[0, octant].astype(F32)
         for part in range(parts):
+            child_copy(part * octants + octant).wait()
 
             def unpack(m, carry, flag=flag, octant=octant, part=part):
                 at = pl.multiple_of((part * octants + octant) * per + 16 * m, 16)
@@ -108,13 +109,13 @@
     for i in range(3):
         tap = row16 + 16 * i - lane16
         bands.append(jnp.where((tap >= 0) & (tap < 8), 1.0, 0.0).astype(BF16))
+    lane_16 = lax.broadcasted_iota(jnp.int32, (16, LANES), 1)
     nothing = jnp.zeros((16, LANES), BF16)
 
     def coarse(index):
         return [
-            spread[pl.ds(pl.multiple_of((part * per + 2 * index + pol) * octants, 8), 8), :]
+            spread[pl.ds(pl.multiple_of((part * per + 2 * index) * octants, 16), 16), :].astype(BF16)
             for part in range(parts)
-            for pol in range(2)
         ]
 
     def chunk(c, carry):
@@ -127,8 +128,8 @@
             far.append([pltpu.roll(v, 64 + HW, 1) for v in values] if i >= 0 else None)
         for i in range(CHUNK):
             windows = (
-                jnp.concatenate([jnp.where(lane < HW, b, h) for b, h in zip(near[i], near[i + 1])], axis=0).astype(BF16),
-                jnp.concatenate([jnp.where(lane < 64 + HW, h, a) for h, a in zip(far[i + 1], far[i + 2])], axis=0).astype(BF16),
+                jnp.concatenate([jnp.where(lane_16 < HW, b, h) for b, h in zip(near[i], near[i + 1])], axis=0),
+                jnp.concatenate([jnp.where(lane_16 < 64 + HW, h, a) for h, a in zip(far[i + 1], far[i + 2])], axis=0),
             )
             base = pl.multiple_of(c * span, span) + 4 * LANES * i
             real = [None] * 8
@@ -138,10 +139,9 @@
                 for tile in range(2):
                     at = pl.ds(base + (2 * half + tile) * LANES, LANES)
                     turned = jnp.take_along_axis(weights_in[:, at], turn, axis=0, mode="promise_in_bounds")
-                    turned = jnp.concatenate([turned, turned], axis=0)
-                    top = turned.astype(BF16)
-                    high.append(top)
-                    low.append((turned - top.astype(F32)).astype(BF16))
+                    rest = turned - turned.astype(BF16).astype(F32)
+                    high.append(jnp.concatenate([turned, turned], axis=0).astype(BF16))
+                    low.append(jnp.concatenate([rest, rest], axis=0).astype(BF16))
                 weights = [
                     jnp.concatenate(
                         [
@@ -166,15 +166,12 @@
                         spot = 2 * (2 * half + tile) + pol
                         real[spot] = re * cos_tile - im * sin_tile
                         imag[spot] = re * sin_tile + im * cos_tile
-            patterns[c * CHUNK + i] = jnp.concatenate([row_sums(real), row_sums(imag)], axis=0).astype(BF16)
-        for g in range(groups):
-            out_copy(c, g).start()
+            pattern = jnp.concatenate([row_sums(real), row_sums(imag)], axis=0).astype(BF16)
+            for g in range(groups):
+                out_ref[g, c * CHUNK + i] = pattern
         return carry
 
     lax.fori_loop(0, chunks, chunk, 0)
-    for c in range(chunks):
-        for g in range(groups):
-            out_copy(c, g).wait()
 
 
 def aggregate(children, present, interp, phase, groups):
@@ -184,21 +181,20 @@
     return pl.pallas_call(
         aggregate_kernel,
         in_specs=[anywhere, anywhere, anywhere, anywhere],
-        out_specs=anywhere,
-        out_shape=jax.ShapeDtypeStruct((groups, total, 16, LANES), BF16),
+        out_specs=pl.BlockSpec(memory_space=pltpu.VMEM),
+        out_shape=pltpu.VMEM((groups, total, 16, LANES), BF16),
         scratch_shapes=[
             pltpu.VMEM(children.shape, BF16),
             pltpu.VMEM(children.shape, F32),
             pltpu.VMEM(interp.shape, F32),
             pltpu.VMEM(phase.shape, F32),
-            pltpu.VMEM((total, 16, LANES), BF16),
             pltpu.SMEM(present.shape, jnp.int32),
-            pltpu.SemaphoreType.DMA,
+            pltpu.SemaphoreType.DMA((16,)),
             pltpu.SemaphoreType.DMA,
             pltpu.SemaphoreType.DMA((chunks,)),
             pltpu.SemaphoreType.DMA((chunks,)),
-            pltpu.SemaphoreType.DMA((chunks, groups)),
         ],
+        compiler_params=pltpu.CompilerParams(vmem_limit_bytes=LIMIT * 1024),
         name="aggregate",
     )(present, children, interp, phase)
 

time: 33.3 us -> 32.1 us (0.964)
  Pallas kernels: 8.06 us -> 7.1 us
    pallas_call x1, Pallas kernels: 5.84 us -> 4.88 us  [aggregate(): pl.pallas_call(aggregate_kernel, in_specs=[anywhere, anywhere, anywhere,...]
where the time goes in v3:
time: 32.1 us; the launch traced here: 32 us
  blocking collectives  24.8 us (77%)
  Pallas kernels  7.1 us (22%)
    all_to_all x1, blocking collectives, local(): lax.all_to_all(pattern.reshape(-1, 16, LANES), ('grp', 'ang'), 0, 0, tile...  24.8 us
    pallas_call x1, Pallas kernels, aggregate(): pl.pallas_call(aggregate_kernel, in_specs=[anywhere, anywhere, anywhere,...  4.88 us
    pallas_call x1, Pallas kernels, translate_local(): pl.pallas_call(translate_kernel, in_specs=[inside] * 5, out_specs=pl.Bloc...  2.22 us

profile of v3, /device:TPU:1, one launch (start us, length us, event | category | flops | bytes accessed | tf_op | source)
XLA Modules:
  0.0 32.0 jit_solution(9198557021734949787)
XLA Ops:
  0.0 0.0 copy-start
  0.0 0.0 copy-start.1
  0.0 0.0 copy-start.2
  0.0 0.0 copy-start.3
  0.0 4.9 %aggregate.1 = bf16[2,64,16,128]{3,2,1,0:T(8,128)(2,1)S(1)} custom-call(s32[1,8]{1,0:T(1,128)} %present_ref.1, bf16[2048,128]{1,0:T(8,128)(2,1)} %bitcast.24, f32[8,32768]{1,0:T(8,128)} %interp_ref.1, f32[8,32768]{1,0:T(8,128)} %phase_ref.1), custom_call_target="tpu_custom_call" | custom-call | tf_op jit(solution)/shard_map/aggregate/pallas_call | solution.py:181
  4.9 24.8 %all_to_all.5 = bf16[128,16,128]{2,1,0:T(8,128)(2,1)S(1)} all-to-all(bf16[128,16,128]{2,1,0:T(8,128)(2,1)S(1)} %bitcast.19), channel_id=1, replica_groups=mesh['grp'=2,'ang'=64] {'grp','ang'}, dimensions={0} | all-to-all | bytes 1048576 | tf_op jit(solution)/shard_map/all_to_all | solution.py:287
  29.7 0.0 copy-done
  29.7 0.0 copy-done.1
  29.8 0.0 copy-done.2
  29.8 0.0 copy-done.3
  29.8 2.2 %translate.1 = f32[2,64,8,128]{3,2,1,0:T(8,128)} custom-call(s32[8,64]{1,0:T(8,128)S(1)} %bitcast.21, s32[8,64]{1,0:T(8,128)S(1)} %bitcast.22, s32[1,64]{1,0:T(1,128)S(1)} %bitcast.23, bf16[2048,128]{1,0:T(8,128)(2,1)S(1)} %bitcast.18, f32[2528,128]{1,0:T(8,128)S(1)} %bitcast.20), custom_call_target="tpu_custom_call" | custom-call | tf_op jit(solution)/shard_map/translate/pallas_call | solution.py:266
Async XLA Ops:
  0.0 29.7 %copy-start = (f32[2,316,512]{2,0,1:T(2,128)S(1)}, f32[2,316,512]{2,0,1:T(2,128)}, u32[]{:S(2)}) copy-start(f32[2,316,512]{2,0,1:T(2,128)} %param.12) | copy-start | bytes 3883012
  0.0 29.7 %copy-start.1 = (s32[64,8]{0,1:T(8,128)S(1)}, s32[64,8]{0,1:T(8,128)}, u32[]{:S(2)}) copy-start(s32[64,8]{0,1:T(8,128)} %param.13) | copy-start | bytes 6148
  0.0 29.7 %copy-start.2 = (s32[64,8]{0,1:T(8,128)S(1)}, s32[64,8]{0,1:T(8,128)}, u32[]{:S(2)}) copy-start(s32[64,8]{0,1:T(8,128)} %param.14) | copy-start | bytes 6148
  0.0 29.7 %copy-start.3 = (s32[64]{0:T(128)S(1)}, s32[64]{0:T(128)}, u32[]{:S(2)}) copy-start(s32[64]{0:T(128)} %param.15) | copy-start | bytes 772

commit v4 on v3

--- a/solution.py
+++ b/solution.py
@@ -206,7 +206,7 @@
 
 
 def translate_kernel(
-    sources_ref, ids_ref, used_ref, pattern_ref, trans_ref, out_ref, places, table, unpacked, received, table_sem, out_sem
+    sources_ref, ids_ref, used_ref, pattern_ref, trans_ref, out_ref, places, table, unpacked, spread_trans, received, table_sem, out_sem
 ):
     slots, receivers = sources_ref.shape
     clusters = pattern_ref.shape[0] // 16
@@ -218,7 +218,7 @@
 
     slot_row = lax.broadcasted_iota(jnp.int32, (slots, receivers), 0)
     places[:slots, :] = jnp.where(slot_row < used_ref[...], sources_ref[...], clusters) * 16
-    places[slots:, :] = ids_ref[...] * 8
+    places[slots:, :] = ids_ref[...] * 16
     table_copy = pltpu.make_async_copy(places, table, table_sem)
     table_copy.start()
 
@@ -232,17 +232,26 @@
     row = lax.broadcasted_iota(jnp.int32, (8, LANES), 0)
     even = (row & 1) == 0
     order = 2 * (row & 3) + (row >> 2)
+
+    def expand(k, carry):
+        operator = trans_ref[pl.ds(pl.multiple_of(8 * k, 8), 8), :]
+        at = pl.multiple_of(16 * k, 16)
+        spread_trans[pl.ds(at, 8), :] = jnp.where(even, operator, pltpu.roll(operator, 1, 0))
+        spread_trans[pl.ds(at + 8, 8), :] = jnp.where(even, pltpu.roll(operator, 7, 0), operator)
+        return carry
+
+    lax.fori_loop(0, trans_ref.shape[0] // 8, expand, 0, unroll=4)
     table_copy.wait()
 
     for receiver in range(receivers):
         real = imag = None
         for slot in range(slots):
             source = pl.multiple_of(table[slot, receiver], 16)
-            operator = trans_ref[pl.ds(pl.multiple_of(table[slots + slot, receiver], 8), 8), :]
+            operator = pl.multiple_of(table[slots + slot, receiver], 16)
             re = unpacked[pl.ds(source, 8), :]
             im = unpacked[pl.ds(source + 8, 8), :]
-            t_re = jnp.where(even, operator, pltpu.roll(operator, 1, 0))
-            t_im = jnp.where(even, pltpu.roll(operator, 7, 0), operator)
+            t_re = spread_trans[pl.ds(operator, 8), :]
+            t_im = spread_trans[pl.ds(operator + 8, 8), :]
             new_re = t_re * re - t_im * im
             new_im = t_re * im + t_im * re
             real = new_re if real is None else real + new_re
@@ -272,6 +281,7 @@
             pltpu.VMEM((2 * slots, receivers), jnp.int32),
             pltpu.SMEM((2 * slots, receivers), jnp.int32),
             pltpu.VMEM((16 * (clusters + 1), LANES), F32),
+            pltpu.VMEM((16 * kinds, LANES), F32),
             pltpu.VMEM((2, receivers, 8, LANES), F32),
             pltpu.SemaphoreType.DMA,
             pltpu.SemaphoreType.DMA((receivers // BATCH,)),

time: 32.1 us -> 31.9 us (level)
  no operation moved by 1% of the time
where the time goes in v4:
time: 31.9 us; the launch traced here: 31.8 us
  blocking collectives  24.8 us (78%)
  Pallas kernels  6.87 us (22%)
    all_to_all x1, blocking collectives, local(): lax.all_to_all(pattern.reshape(-1, 16, LANES), ('grp', 'ang'), 0, 0, tile...  24.8 us
    pallas_call x1, Pallas kernels, aggregate(): pl.pallas_call(aggregate_kernel, in_specs=[anywhere, anywhere, anywhere,...  4.88 us
    pallas_call x1, Pallas kernels, translate_local(): pl.pallas_call(translate_kernel, in_specs=[inside] * 5, out_specs=pl.Bloc...  2 us

profile of v4, /device:TPU:1, one launch (start us, length us, event | category | flops | bytes accessed | tf_op | source)
XLA Modules:
  0.0 31.8 jit_solution(10592271515959420401)
XLA Ops:
  0.0 0.0 copy-start
  0.0 0.0 copy-start.1
  0.0 0.0 copy-start.2
  0.0 0.0 copy-start.3
  0.0 4.9 %aggregate.1 = bf16[2,64,16,128]{3,2,1,0:T(8,128)(2,1)S(1)} custom-call(s32[1,8]{1,0:T(1,128)} %present_ref.1, bf16[2048,128]{1,0:T(8,128)(2,1)} %bitcast.24, f32[8,32768]{1,0:T(8,128)} %interp_ref.1, f32[8,32768]{1,0:T(8,128)} %phase_ref.1), custom_call_target="tpu_custom_call" | custom-call | tf_op jit(solution)/shard_map/aggregate/pallas_call | solution.py:181
  4.9 24.8 %all_to_all.5 = bf16[128,16,128]{2,1,0:T(8,128)(2,1)S(1)} all-to-all(bf16[128,16,128]{2,1,0:T(8,128)(2,1)S(1)} %bitcast.19), channel_id=1, replica_groups=mesh['grp'=2,'ang'=64] {'grp','ang'}, dimensions={0} | all-to-all | bytes 1048576 | tf_op jit(solution)/shard_map/all_to_all | solution.py:297
  29.7 0.0 copy-done
  29.7 0.0 copy-done.1
  29.8 0.0 copy-done.2
  29.8 0.0 copy-done.3
  29.8 2.0 %translate.1 = f32[2,64,8,128]{3,2,1,0:T(8,128)} custom-call(s32[8,64]{1,0:T(8,128)S(1)} %bitcast.21, s32[8,64]{1,0:T(8,128)S(1)} %bitcast.22, s32[1,64]{1,0:T(1,128)S(1)} %bitcast.23, bf16[2048,128]{1,0:T(8,128)(2,1)S(1)} %bitcast.18, f32[2528,128]{1,0:T(8,128)S(1)} %bitcast.20), custom_call_target="tpu_custom_call" | custom-call | tf_op jit(solution)/shard_map/translate/pallas_call | solution.py:275
Async XLA Ops:
  0.0 29.7 %copy-start = (f32[2,316,512]{2,0,1:T(2,128)S(1)}, f32[2,316,512]{2,0,1:T(2,128)}, u32[]{:S(2)}) copy-start(f32[2,316,512]{2,0,1:T(2,128)} %param.12) | copy-start | bytes 3883012
  0.0 29.7 %copy-start.1 = (s32[64,8]{0,1:T(8,128)S(1)}, s32[64,8]{0,1:T(8,128)}, u32[]{:S(2)}) copy-start(s32[64,8]{0,1:T(8,128)} %param.13) | copy-start | bytes 6148
  0.0 29.7 %copy-start.2 = (s32[64,8]{0,1:T(8,128)S(1)}, s32[64,8]{0,1:T(8,128)}, u32[]{:S(2)}) copy-start(s32[64,8]{0,1:T(8,128)} %param.14) | copy-start | bytes 6148
  0.0 29.7 %copy-start.3 = (s32[64]{0:T(128)S(1)}, s32[64]{0:T(128)}, u32[]{:S(2)}) copy-start(s32[64]{0:T(128)} %param.15) | copy-start | bytes 772

commit v5 on v4

--- a/solution.py
+++ b/solution.py
@@ -10,6 +10,7 @@
 HW = 4
 LANES = 128
 CHUNK = 32
+AGAIN = 72
 LIMIT = 57000
 BATCH = 8
 F32 = jnp.float32
@@ -105,32 +106,44 @@
     turn = (row - lane // 4) & 7
     row16 = lax.broadcasted_iota(jnp.int32, (16, LANES), 0)
     lane16 = lax.broadcasted_iota(jnp.int32, (16, LANES), 1) // 4
-    bands = []
-    for i in range(3):
-        tap = row16 + 16 * i - lane16
-        bands.append(jnp.where((tap >= 0) & (tap < 8), 1.0, 0.0).astype(BF16))
+    def bands(first):
+        taps = [row16 + 16 * i - first - lane16 for i in range(3)]
+        return [jnp.where((tap >= 0) & (tap < 8), 1.0, 0.0).astype(BF16) for tap in taps]
+
+    high_bands, low_bands = bands(0), bands(8)
     lane_16 = lax.broadcasted_iota(jnp.int32, (16, LANES), 1)
     nothing = jnp.zeros((16, LANES), BF16)
 
-    def coarse(index):
-        return [
+    shifts = (HW, HW + AGAIN, LANES // 2 + HW, LANES // 2 + HW + AGAIN - LANES)
+
+    def shifted(index):
+        tiles = [
             spread[pl.ds(pl.multiple_of((part * per + 2 * index) * octants, 16), 16), :].astype(BF16)
             for part in range(parts)
         ]
+        return [[pltpu.roll(t, shift, 1) for shift in shifts] for t in tiles]
+
+    def windows_of(before, now, after):
+        first, second = [], []
+        for part in range(parts):
+            near, near_again, far, far_again = now[part]
+            left = jnp.where(
+                lane_16 < HW,
+                before[part][0],
+                jnp.where(lane_16 < AGAIN, near, jnp.where(lane_16 < AGAIN + HW, before[part][1], near_again)),
+            )
+            first.append(jnp.concatenate([left, near_again], axis=1))
+            left = jnp.where(lane_16 < shifts[2], far, jnp.where(lane_16 < AGAIN, after[part][2], far_again))
+            right = jnp.where(lane_16 < shifts[3], far_again, after[part][3])
+            second.append(jnp.concatenate([left, right], axis=1))
+        return jnp.concatenate(first, axis=0), jnp.concatenate(second, axis=0)
 
     def chunk(c, carry):
         weight_copy(c).wait()
         phase_copy(c).wait()
-        near, far = [], []
-        for i in range(-1, CHUNK + 1):
-            values = coarse(lax.rem(c * CHUNK + i + total, total))
-            near.append([pltpu.roll(v, HW, 1) for v in values] if i < CHUNK else None)
-            far.append([pltpu.roll(v, 64 + HW, 1) for v in values] if i >= 0 else None)
+        moved = [shifted(lax.rem(c * CHUNK + i + total, total)) for i in range(-1, CHUNK + 1)]
         for i in range(CHUNK):
-            windows = (
-                jnp.concatenate([jnp.where(lane_16 < HW, b, h) for b, h in zip(near[i], near[i + 1])], axis=0),
-                jnp.concatenate([jnp.where(lane_16 < 64 + HW, h, a) for h, a in zip(far[i + 1], far[i + 2])], axis=0),
-            )
+            windows = windows_of(*moved[i : i + 3])
             base = pl.multiple_of(c * span, span) + 4 * LANES * i
             real = [None] * 8
             imag = [None] * 8
@@ -142,19 +155,18 @@
                     rest = turned - turned.astype(BF16).astype(F32)
                     high.append(jnp.concatenate([turned, turned], axis=0).astype(BF16))
                     low.append(jnp.concatenate([rest, rest], axis=0).astype(BF16))
-                weights = [
-                    jnp.concatenate(
-                        [
-                            jnp.concatenate([left * b for b in bands] + [nothing] * 5, axis=0),
-                            jnp.concatenate([nothing] * 2 + [right * b for b in bands] + [nothing] * 3, axis=0),
-                        ],
-                        axis=1,
-                    )
-                    for left, right in (high, low)
-                ]
+                left, right = ([part * b for b in high_bands] for part in high)
+                left_low, right_low = ([part * b for b in low_bands] for part in low)
+                weights = jnp.concatenate(
+                    [
+                        jnp.concatenate(left + [nothing] + left_low + [nothing] * 9, axis=0),
+                        jnp.concatenate([nothing] * 2 + right + [nothing] + right_low + [nothing] * 7, axis=0),
+                    ],
+                    axis=1,
+                )
                 refined = jnp.dot(
-                    jnp.concatenate([windows[half], windows[half]], axis=1),
-                    jnp.concatenate(weights, axis=0),
+                    windows[half],
+                    weights,
                     preferred_element_type=F32,
                 )
                 for tile in range(2):

time: 31.9 us -> 31.3 us (0.981)
  Pallas kernels: 6.87 us -> 6.24 us
    pallas_call x1, Pallas kernels: 4.88 us -> 4.25 us  [aggregate(): pl.pallas_call(aggregate_kernel, in_specs=[anywhere, anywhere, anywhere,...]
where the time goes in v5:
time: 31.3 us; the launch traced here: 31.1 us
  blocking collectives  24.8 us (79%)
  Pallas kernels  6.24 us (20%)
    all_to_all x1, blocking collectives, local(): lax.all_to_all(pattern.reshape(-1, 16, LANES), ('grp', 'ang'), 0, 0, tile...  24.8 us
    pallas_call x1, Pallas kernels, aggregate(): pl.pallas_call(aggregate_kernel, in_specs=[anywhere, anywhere, anywhere,...  4.25 us
    pallas_call x1, Pallas kernels, translate_local(): pl.pallas_call(translate_kernel, in_specs=[inside] * 5, out_specs=pl.Bloc...  2 us

profile of v5, /device:TPU:1, one launch (start us, length us, event | category | flops | bytes accessed | tf_op | source)
XLA Modules:
  0.0 31.1 jit_solution(9697224131681077088)
XLA Ops:
  0.0 0.0 copy-start
  0.0 0.0 copy-start.1
  0.0 0.0 copy-start.2
  0.0 0.0 copy-start.3
  0.0 4.2 %aggregate.1 = bf16[2,64,16,128]{3,2,1,0:T(8,128)(2,1)S(1)} custom-call(s32[1,8]{1,0:T(1,128)} %present_ref.1, bf16[2048,128]{1,0:T(8,128)(2,1)} %bitcast.24, f32[8,32768]{1,0:T(8,128)} %interp_ref.1, f32[8,32768]{1,0:T(8,128)} %phase_ref.1), custom_call_target="tpu_custom_call" | custom-call | tf_op jit(solution)/shard_map/aggregate/pallas_call | solution.py:193
  4.3 24.8 %all_to_all.5 = bf16[128,16,128]{2,1,0:T(8,128)(2,1)S(1)} all-to-all(bf16[128,16,128]{2,1,0:T(8,128)(2,1)S(1)} %bitcast.19), channel_id=1, replica_groups=mesh['grp'=2,'ang'=64] {'grp','ang'}, dimensions={0} | all-to-all | bytes 1048576 | tf_op jit(solution)/shard_map/all_to_all | solution.py:309
  29.1 0.0 copy-done
  29.1 0.0 copy-done.1
  29.1 0.0 copy-done.2
  29.1 0.0 copy-done.3
  29.1 2.0 %translate.1 = f32[2,64,8,128]{3,2,1,0:T(8,128)} custom-call(s32[8,64]{1,0:T(8,128)S(1)} %bitcast.21, s32[8,64]{1,0:T(8,128)S(1)} %bitcast.22, s32[1,64]{1,0:T(1,128)S(1)} %bitcast.23, bf16[2048,128]{1,0:T(8,128)(2,1)S(1)} %bitcast.18, f32[2528,128]{1,0:T(8,128)S(1)} %bitcast.20), custom_call_target="tpu_custom_call" | custom-call | tf_op jit(solution)/shard_map/translate/pallas_call | solution.py:287
Async XLA Ops:
  0.0 29.1 %copy-start = (f32[2,316,512]{2,0,1:T(2,128)S(1)}, f32[2,316,512]{2,0,1:T(2,128)}, u32[]{:S(2)}) copy-start(f32[2,316,512]{2,0,1:T(2,128)} %param.12) | copy-start | bytes 3883012
  0.0 29.1 %copy-start.1 = (s32[64,8]{0,1:T(8,128)S(1)}, s32[64,8]{0,1:T(8,128)}, u32[]{:S(2)}) copy-start(s32[64,8]{0,1:T(8,128)} %param.13) | copy-start | bytes 6148
  0.0 29.1 %copy-start.2 = (s32[64,8]{0,1:T(8,128)S(1)}, s32[64,8]{0,1:T(8,128)}, u32[]{:S(2)}) copy-start(s32[64,8]{0,1:T(8,128)} %param.14) | copy-start | bytes 6148
  0.0 29.1 %copy-start.3 = (s32[64]{0:T(128)S(1)}, s32[64]{0:T(128)}, u32[]{:S(2)}) copy-start(s32[64]{0:T(128)} %param.15) | copy-start | bytes 772

commit v6 on v5

--- a/solution.py
+++ b/solution.py
@@ -121,19 +121,22 @@
             spread[pl.ds(pl.multiple_of((part * per + 2 * index) * octants, 16), 16), :].astype(BF16)
             for part in range(parts)
         ]
-        return [[pltpu.roll(t, shift, 1) for shift in shifts] for t in tiles]
+        moved = []
+        for tile in tiles:
+            near, near_again, far, far_again = (pltpu.roll(tile, shift, 1) for shift in shifts)
+            once = lane_16 < AGAIN
+            moved.append((jnp.where(once, near, near_again), near_again, jnp.where(once, far, far_again), far_again))
+        return moved
+
+    from_before = (lane_16 < HW) | ((lane_16 >= AGAIN) & (lane_16 < AGAIN + HW))
+    from_after = (lane_16 >= shifts[2]) & (lane_16 < AGAIN)
 
     def windows_of(before, now, after):
         first, second = [], []
         for part in range(parts):
             near, near_again, far, far_again = now[part]
-            left = jnp.where(
-                lane_16 < HW,
-                before[part][0],
-                jnp.where(lane_16 < AGAIN, near, jnp.where(lane_16 < AGAIN + HW, before[part][1], near_again)),
-            )
-            first.append(jnp.concatenate([left, near_again], axis=1))
-            left = jnp.where(lane_16 < shifts[2], far, jnp.where(lane_16 < AGAIN, after[part][2], far_again))
+            first.append(jnp.concatenate([jnp.where(from_before, before[part][0], near), near_again], axis=1))
+            left = jnp.where(from_after, after[part][2], far)
             right = jnp.where(lane_16 < shifts[3], far_again, after[part][3])
             second.append(jnp.concatenate([left, right], axis=1))
         return jnp.concatenate(first, axis=0), jnp.concatenate(second, axis=0)

time: 31.3 us -> 31.1 us (level)
  no operation moved by 1% of the time
where the time goes in v6:
time: 31.1 us; the launch traced here: 31 us
  blocking collectives  24.8 us (80%)
  Pallas kernels  6.11 us (20%)
    all_to_all x1, blocking collectives, local(): lax.all_to_all(pattern.reshape(-1, 16, LANES), ('grp', 'ang'), 0, 0, tile...  24.8 us
    pallas_call x1, Pallas kernels, aggregate(): pl.pallas_call(aggregate_kernel, in_specs=[anywhere, anywhere, anywhere,...  4.12 us
    pallas_call x1, Pallas kernels, translate_local(): pl.pallas_call(translate_kernel, in_specs=[inside] * 5, out_specs=pl.Bloc...  2 us

profile of v6, /device:TPU:1, one launch (start us, length us, event | category | flops | bytes accessed | tf_op | source)
XLA Modules:
  0.0 31.0 jit_solution(15585864970876804893)
XLA Ops:
  0.0 0.0 copy-start
  0.0 0.0 copy-start.1
  0.0 0.0 copy-start.2
  0.0 0.0 copy-start.3
  0.0 4.1 %aggregate.1 = bf16[2,64,16,128]{3,2,1,0:T(8,128)(2,1)S(1)} custom-call(s32[1,8]{1,0:T(1,128)} %present_ref.1, bf16[2048,128]{1,0:T(8,128)(2,1)} %bitcast.24, f32[8,32768]{1,0:T(8,128)} %interp_ref.1, f32[8,32768]{1,0:T(8,128)} %phase_ref.1), custom_call_target="tpu_custom_call" | custom-call | tf_op jit(solution)/shard_map/aggregate/pallas_call | solution.py:196
  4.1 24.8 %all_to_all.5 = bf16[128,16,128]{2,1,0:T(8,128)(2,1)S(1)} all-to-all(bf16[128,16,128]{2,1,0:T(8,128)(2,1)S(1)} %bitcast.19), channel_id=1, replica_groups=mesh['grp'=2,'ang'=64] {'grp','ang'}, dimensions={0} | all-to-all | bytes 1048576 | tf_op jit(solution)/shard_map/all_to_all | solution.py:312
  29.0 0.0 copy-done
  29.0 0.0 copy-done.1
  29.0 0.0 copy-done.2
  29.0 0.0 copy-done.3
  29.0 2.0 %translate.1 = f32[2,64,8,128]{3,2,1,0:T(8,128)} custom-call(s32[8,64]{1,0:T(8,128)S(1)} %bitcast.21, s32[8,64]{1,0:T(8,128)S(1)} %bitcast.22, s32[1,64]{1,0:T(1,128)S(1)} %bitcast.23, bf16[2048,128]{1,0:T(8,128)(2,1)S(1)} %bitcast.18, f32[2528,128]{1,0:T(8,128)S(1)} %bitcast.20), custom_call_target="tpu_custom_call" | custom-call | tf_op jit(solution)/shard_map/translate/pallas_call | solution.py:290
Async XLA Ops:
  0.0 29.0 %copy-start = (f32[2,316,512]{2,0,1:T(2,128)S(1)}, f32[2,316,512]{2,0,1:T(2,128)}, u32[]{:S(2)}) copy-start(f32[2,316,512]{2,0,1:T(2,128)} %param.12) | copy-start | bytes 3883012
  0.0 29.0 %copy-start.1 = (s32[64,8]{0,1:T(8,128)S(1)}, s32[64,8]{0,1:T(8,128)}, u32[]{:S(2)}) copy-start(s32[64,8]{0,1:T(8,128)} %param.13) | copy-start | bytes 6148
  0.0 29.0 %copy-start.2 = (s32[64,8]{0,1:T(8,128)S(1)}, s32[64,8]{0,1:T(8,128)}, u32[]{:S(2)}) copy-start(s32[64,8]{0,1:T(8,128)} %param.14) | copy-start | bytes 6148
  0.0 29.0 %copy-start.3 = (s32[64]{0:T(128)S(1)}, s32[64]{0:T(128)}, u32[]{:S(2)}) copy-start(s32[64]{0:T(128)} %param.15) | copy-start | bytes 772

commit v7 on v6

--- a/solution.py
+++ b/solution.py
@@ -45,7 +45,8 @@
 
 def row_sums(rows):
     place = lax.broadcasted_iota(jnp.int32, rows[0].shape, 0)
-    for distance in (1, 2, 4):
+    rows = [a + pltpu.roll(b, 1, 0) for a, b in zip(rows[0::2], rows[1::2])]
+    for distance in (2, 4):
         first = (place & distance) == 0
         rows = [
             jnp.where(first, a, b) + pltpu.roll(jnp.where(first, b, a), distance, 0)
@@ -86,6 +87,7 @@
         phase_copy(c).start()
     flag_copy.wait()
 
+    other = lax.broadcasted_iota(jnp.int32, (8, LANES), 0) ^ 1
     for octant in range(octants):
         flag = flags[0, octant].astype(F32)
         for part in range(parts):
@@ -95,8 +97,11 @@
                 at = pl.multiple_of((part * octants + octant) * per + 16 * m, 16)
                 rows = stored[pl.ds(at, 16), :].astype(F32) * flag
                 to = (part * per + 16 * m) * octants + octant
-                spread[pl.ds(to, 8, stride=octants), :] = rows[:8]
-                spread[pl.ds(to + 8 * octants, 8, stride=octants), :] = rows[8:]
+                for n in range(2):
+                    these = rows[8 * n : 8 * n + 8]
+                    if octant % 2:
+                        these = jnp.take_along_axis(these, other, axis=0, mode="promise_in_bounds")
+                    spread[pl.ds(to + 8 * n * octants, 8, stride=octants), :] = these
                 return carry
 
             lax.fori_loop(0, per // 16, unpack, 0, unroll=True)

time: 31.1 us -> 31 us (level)
  no operation moved by 1% of the time
where the time goes in v7:
time: 31 us; the launch traced here: 30.9 us
  blocking collectives  24.8 us (80%)
  Pallas kernels  5.99 us (19%)
    all_to_all x1, blocking collectives, local(): lax.all_to_all(pattern.reshape(-1, 16, LANES), ('grp', 'ang'), 0, 0, tile...  24.8 us
    pallas_call x1, Pallas kernels, aggregate(): pl.pallas_call(aggregate_kernel, in_specs=[anywhere, anywhere, anywhere,...  3.99 us
    pallas_call x1, Pallas kernels, translate_local(): pl.pallas_call(translate_kernel, in_specs=[inside] * 5, out_specs=pl.Bloc...  2 us

profile of v7, /device:TPU:1, one launch (start us, length us, event | category | flops | bytes accessed | tf_op | source)
XLA Modules:
  0.0 30.9 jit_solution(1231383791152722693)
XLA Ops:
  0.0 0.0 copy-start
  0.0 0.0 copy-start.1
  0.0 0.0 copy-start.2
  0.0 0.0 copy-start.3
  0.0 4.0 %aggregate.1 = bf16[2,64,16,128]{3,2,1,0:T(8,128)(2,1)S(1)} custom-call(s32[1,8]{1,0:T(1,128)} %present_ref.1, bf16[2048,128]{1,0:T(8,128)(2,1)} %bitcast.24, f32[8,32768]{1,0:T(8,128)} %interp_ref.1, f32[8,32768]{1,0:T(8,128)} %phase_ref.1), custom_call_target="tpu_custom_call" | custom-call | tf_op jit(solution)/shard_map/aggregate/pallas_call | solution.py:201
  4.0 24.8 %all_to_all.5 = bf16[128,16,128]{2,1,0:T(8,128)(2,1)S(1)} all-to-all(bf16[128,16,128]{2,1,0:T(8,128)(2,1)S(1)} %bitcast.19), channel_id=1, replica_groups=mesh['grp'=2,'ang'=64] {'grp','ang'}, dimensions={0} | all-to-all | bytes 1048576 | tf_op jit(solution)/shard_map/all_to_all | solution.py:317
  28.9 0.0 copy-done
  28.9 0.0 copy-done.1
  28.9 0.0 copy-done.2
  28.9 0.0 copy-done.3
  28.9 2.0 %translate.1 = f32[2,64,8,128]{3,2,1,0:T(8,128)} custom-call(s32[8,64]{1,0:T(8,128)S(1)} %bitcast.21, s32[8,64]{1,0:T(8,128)S(1)} %bitcast.22, s32[1,64]{1,0:T(1,128)S(1)} %bitcast.23, bf16[2048,128]{1,0:T(8,128)(2,1)S(1)} %bitcast.18, f32[2528,128]{1,0:T(8,128)S(1)} %bitcast.20), custom_call_target="tpu_custom_call" | custom-call | tf_op jit(solution)/shard_map/translate/pallas_call | solution.py:295
Async XLA Ops:
  0.0 28.9 %copy-start = (f32[2,316,512]{2,0,1:T(2,128)S(1)}, f32[2,316,512]{2,0,1:T(2,128)}, u32[]{:S(2)}) copy-start(f32[2,316,512]{2,0,1:T(2,128)} %param.12) | copy-start | bytes 3883012
  0.0 28.9 %copy-start.1 = (s32[64,8]{0,1:T(8,128)S(1)}, s32[64,8]{0,1:T(8,128)}, u32[]{:S(2)}) copy-start(s32[64,8]{0,1:T(8,128)} %param.13) | copy-start | bytes 6148
  0.0 28.9 %copy-start.2 = (s32[64,8]{0,1:T(8,128)S(1)}, s32[64,8]{0,1:T(8,128)}, u32[]{:S(2)}) copy-start(s32[64,8]{0,1:T(8,128)} %param.14) | copy-start | bytes 6148
  0.0 28.9 %copy-start.3 = (s32[64]{0:T(128)S(1)}, s32[64]{0:T(128)}, u32[]{:S(2)}) copy-start(s32[64]{0:T(128)} %param.15) | copy-start | bytes 772

commit v8 on v7

--- a/solution.py
+++ b/solution.py
@@ -260,7 +260,7 @@
         spread_trans[pl.ds(at + 8, 8), :] = jnp.where(even, pltpu.roll(operator, 7, 0), operator)
         return carry
 
-    lax.fori_loop(0, trans_ref.shape[0] // 8, expand, 0, unroll=4)
+    lax.fori_loop(0, trans_ref.shape[0] // 8, expand, 0, unroll=79)
     table_copy.wait()
 
     for receiver in range(receivers):

time: 31 us -> 31 us (level)
  no operation moved by 1% of the time
where the time goes in v8:
time: 31 us; the launch traced here: 30.8 us
  blocking collectives  24.8 us (80%)
  Pallas kernels  5.94 us (19%)
    all_to_all x1, blocking collectives, local(): lax.all_to_all(pattern.reshape(-1, 16, LANES), ('grp', 'ang'), 0, 0, tile...  24.8 us
    pallas_call x1, Pallas kernels, aggregate(): pl.pallas_call(aggregate_kernel, in_specs=[anywhere, anywhere, anywhere,...  3.99 us
    pallas_call x1, Pallas kernels, translate_local(): pl.pallas_call(translate_kernel, in_specs=[inside] * 5, out_specs=pl.Bloc...  1.94 us

profile of v8, /device:TPU:1, one launch (start us, length us, event | category | flops | bytes accessed | tf_op | source)
XLA Modules:
  0.0 30.8 jit_solution(6120922767306532855)
XLA Ops:
  0.0 0.0 copy-start
  0.0 0.0 copy-start.1
  0.0 0.0 copy-start.2
  0.0 0.0 copy-start.3
  0.0 4.0 %aggregate.1 = bf16[2,64,16,128]{3,2,1,0:T(8,128)(2,1)S(1)} custom-call(s32[1,8]{1,0:T(1,128)} %present_ref.1, bf16[2048,128]{1,0:T(8,128)(2,1)} %bitcast.24, f32[8,32768]{1,0:T(8,128)} %interp_ref.1, f32[8,32768]{1,0:T(8,128)} %phase_ref.1), custom_call_target="tpu_custom_call" | custom-call | tf_op jit(solution)/shard_map/aggregate/pallas_call | solution.py:201
  4.0 24.8 %all_to_all.5 = bf16[128,16,128]{2,1,0:T(8,128)(2,1)S(1)} all-to-all(bf16[128,16,128]{2,1,0:T(8,128)(2,1)S(1)} %bitcast.19), channel_id=1, replica_groups=mesh['grp'=2,'ang'=64] {'grp','ang'}, dimensions={0} | all-to-all | bytes 1048576 | tf_op jit(solution)/shard_map/all_to_all | solution.py:317
  28.9 0.0 copy-done
  28.9 0.0 copy-done.1
  28.9 0.0 copy-done.2
  28.9 0.0 copy-done.3
  28.9 1.9 %translate.1 = f32[2,64,8,128]{3,2,1,0:T(8,128)} custom-call(s32[8,64]{1,0:T(8,128)S(1)} %bitcast.21, s32[8,64]{1,0:T(8,128)S(1)} %bitcast.22, s32[1,64]{1,0:T(1,128)S(1)} %bitcast.23, bf16[2048,128]{1,0:T(8,128)(2,1)S(1)} %bitcast.18, f32[2528,128]{1,0:T(8,128)S(1)} %bitcast.20), custom_call_target="tpu_custom_call" | custom-call | tf_op jit(solution)/shard_map/translate/pallas_call | solution.py:295
Async XLA Ops:
  0.0 28.9 %copy-start = (f32[2,316,512]{2,0,1:T(2,128)S(1)}, f32[2,316,512]{2,0,1:T(2,128)}, u32[]{:S(2)}) copy-start(f32[2,316,512]{2,0,1:T(2,128)} %param.12) | copy-start | bytes 3883012
  0.0 28.9 %copy-start.1 = (s32[64,8]{0,1:T(8,128)S(1)}, s32[64,8]{0,1:T(8,128)}, u32[]{:S(2)}) copy-start(s32[64,8]{0,1:T(8,128)} %param.13) | copy-start | bytes 6148
  0.0 28.9 %copy-start.2 = (s32[64,8]{0,1:T(8,128)S(1)}, s32[64,8]{0,1:T(8,128)}, u32[]{:S(2)}) copy-start(s32[64,8]{0,1:T(8,128)} %param.14) | copy-start | bytes 6148
  0.0 28.9 %copy-start.3 = (s32[64]{0:T(128)S(1)}, s32[64]{0:T(128)}, u32[]{:S(2)}) copy-start(s32[64]{0:T(128)} %param.15) | copy-start | bytes 772
